TPU v7x, 512 devices: a whole 4x8x8 slice. The times are simulated.
512 devices in a mesh: gx: 8 (over x, core), gy: 8 (over y), gz: 8 (over z).
Axes of the slice: x: 4, y: 8, z: 8, core: 2. Of those that a mesh axis runs over, the one named last changes fastest.
Arguments:
- warped_image: float32 [512, 512, 1024], P('gx', 'gy', 'gz'), may hold values from -6 to 6
- fixed_image: float32 [512, 512, 1024], P('gx', 'gy', 'gz'), may hold values from -6 to 6
- fine_control: float32 [3, 64, 64, 128], P(None, 'gx', 'gy', 'gz'), may hold values from -6 to 6
- coarse_control: float32 [3, 16, 16, 32], replicated, may hold values from -6 to 6
Outputs:
- fine_gradient: float32 [3, 64, 64, 128], P(None, 'gx', 'gy', 'gz')
- coarse_gradient: float32 [3, 16, 16, 32], replicated
All inputs are finite; a program needn't handle non-finite values.
Results may differ from a plain program's by a relative error of at most 0.0003.
Values sent between devices are 32-bit elements; how exact they have to be, the bound alone decides.
No kernel may reach another device: no remote copies, remote signals or barrier semaphores. Data moves between devices by JAX's collectives and lax.ppermute only.
A program may use at most 64 MiB of HBM per device.

v0:
```python
import functools

import jax
import jax.numpy as jnp
import numpy as np
from jax import lax
from jax.experimental import pallas as pl
from jax.experimental.pallas import tpu as pltpu
from jax.sharding import PartitionSpec as P

SPF = 8
SPC = 32
BEND = 0.01
f32 = jnp.float32
bf16 = jnp.bfloat16
VMEM = pltpu.VMEM


def spline(t):
    t = np.abs(t)
    inner = 2.0 / 3.0 - t * t + 0.5 * t**3
    outer = (2.0 - t) ** 3 / 6.0
    return np.where(t < 1.0, inner, np.where(t < 2.0, outer, 0.0))


def weights(voxels, points, spacing):
    centre = (np.arange(points) - 2) * spacing + spacing / 2
    return spline((np.asarray(voxels)[:, None] + 0.5 - centre[None, :]) / spacing)


def halves(matrix):
    matrix = np.asarray(matrix, np.float32)
    high = matrix.astype(bf16)
    return high, (matrix - high.astype(np.float32)).astype(bf16)


def split(values):
    high = values.astype(bf16)
    return high, (values - high.astype(f32)).astype(bf16)


def mm(a, b):
    return jnp.dot(a, b, preferred_element_type=f32)


def mm3(values, high, low):
    a, b = split(values)
    return mm(a, high) + mm(b, high) + mm(a, low)


def lanes(shape):
    return lax.broadcasted_iota(jnp.int32, shape, len(shape) - 1)


def rows_of(shape):
    return lax.broadcasted_iota(jnp.int32, shape, len(shape) - 2)


def rolled(values, shift):
    shift %= values.shape[-1]
    return values if shift == 0 else pltpu.roll(values, shift, values.ndim - 1)


def within(mib):
    return pltpu.CompilerParams(vmem_limit_bytes=mib * 2**20)


def whole(n):
    return [pl.BlockSpec(memory_space=VMEM)] * n


PARTS = ((0, 4), (4, 12), (16, 16), (32, 16), (48, 16))


def faces_kernel(w_hbm, f_hbm, xf_ref, xo_ref, yf_ref, yo_ref, zf_ref, zo_ref, s_ref, t_ref, d_ref, w_ref, f_ref, sem):
    def copies(g):
        part = pl.ds(*PARTS[g])
        return [
            pltpu.make_async_copy(hbm.at[part], ref.at[part], sem.at[i, g])
            for i, (hbm, ref) in enumerate(((w_hbm, w_ref), (f_hbm, f_ref)))
        ]

    for g in range(len(PARTS)):
        for copy in copies(g):
            copy.start()
    lane = lanes((64, 128))
    for ref in (s_ref, t_ref):
        ref[:, 0:8, :] = jnp.zeros((68, 8, 128), f32)
        ref[:, 72:80, :] = jnp.zeros((68, 8, 128), f32)
        for x in (0, 1, 66, 67):
            ref[x, 8:72, :] = jnp.zeros((64, 128), f32)

    for g, (start, size) in enumerate(PARTS):
        for copy in copies(g):
            copy.wait()
        for x in range(start, start + size):
            w = w_ref[x]
            f = f_ref[x]
            s = w + f
            d = w - f
            s_ref[x + 2, 8:72, :] = s
            t_ref[x + 2, 8:72, :] = 8.0 * s
            d_ref[x] = d
            for j in range(2):
                yf_ref[j, x : x + 1, :] = s[62 + j : 63 + j]
                yf_ref[2 + j, x : x + 1, :] = d[62 + j : 63 + j]
                yo_ref[j, x : x + 1, :] = s[j : j + 1]
                yo_ref[2 + j, x : x + 1, :] = d[j : j + 1]
            i = x % 32
            here = (lane >= 4 * i) & (lane < 4 * i + 4)
            packed_s = rolled(s, 4 * i + 2) if i == 0 else jnp.where(here, rolled(s, 4 * i + 2), packed_s)
            packed_d = rolled(d, 4 * i + 2) if i == 0 else jnp.where(here, rolled(d, 4 * i + 2), packed_d)
            if i == 31:
                zo_ref[x // 32] = packed_s
                zo_ref[2 + x // 32] = packed_d

    for j in range(2):
        xf_ref[j] = s_ref[64 + j, 8:72, :]
        xf_ref[2 + j] = d_ref[62 + j]
        xo_ref[j] = s_ref[2 + j, 8:72, :]
        xo_ref[2 + j] = d_ref[j]
        zf_ref[j] = jnp.where(lane % 4 < 2, zo_ref[2 * j], rolled(zo_ref[2 * j + 1], 2))


def faces(w, f):
    shapes = [(4, 64, 128)] * 4 + [(2, 64, 128), (4, 64, 128)] + [(68, 80, 128)] * 2 + [(64, 64, 128)]
    return pl.pallas_call(
        faces_kernel,
        in_specs=[pl.BlockSpec(memory_space=pltpu.HBM)] * 2,
        out_specs=whole(9),
        out_shape=[jax.ShapeDtypeStruct(s, f32) for s in shapes],
        scratch_shapes=[
            VMEM((64, 64, 128), f32),
            VMEM((64, 64, 128), f32),
            pltpu.SemaphoreType.DMA((2, len(PARTS))),
        ],
        compiler_params=within(16),
        name="faces",
    )(*(pltpu.with_memory_space_constraint(v, pltpu.HBM) for v in (w, f)))


def bend_kernel(sizes, c_ref, k_ref, bf_ref, bk_ref, u_ref, k2_ref):
    nx, ny, nz = sizes
    ix, iy, iz = (lax.axis_index(n) for n in ("gx", "gy", "gz"))
    u_ref[...] = jnp.zeros_like(u_ref)
    for a in range(3):
        for p in range(8):
            at = 20 * (p + 2) + 2
            u_ref[a * 16 + 2 : a * 16 + 10, at : at + 16] = c_ref[a, p]
    lane = lanes((48, 256))
    row = rows_of((48, 256)) % 16
    gp = lane // 20 - 2 + 8 * ix
    gr = lane % 20 - 2 + 16 * iz
    gq = row - 2 + 8 * iy
    inside = (gp >= 0) & (gp < 8 * nx) & (gq >= 0) & (gq < 8 * ny) & (gr >= 0) & (gr < 16 * nz)

    def around(u, step):
        total = pltpu.roll(u, 1, 0) + pltpu.roll(u, u.shape[0] - 1, 0)
        for shift in (1, -1, step, -step):
            total = total + rolled(u, shift)
        return total - 6.0 * u

    u = around(u_ref[...], 20)
    u = around(jnp.where(inside, u, 0.0), 20) * BEND
    keep = lanes((48, 128)) < 120
    bf_ref[:, 0:128] = jnp.where(keep, u[:, 0:128], 0.0)
    bf_ref[:, 128:256] = jnp.where(keep, pltpu.roll(u, 136, 1)[:, 0:128], 0.0)

    kx, ky, kz = 2 * nx, 2 * ny, 4 * nz
    k2_ref[...] = jnp.zeros_like(k2_ref)
    parts = []
    for a in range(3):
        total = None
        for p in range(6):
            i = 6 * a + p
            k2_ref[i, 0:ky, 0:kz] = k_ref[a, jnp.clip(2 * ix - 2 + p, 0, kx - 1)]
            tile = pltpu.roll(k2_ref[i], (18 - 2 * iy) % 16, 0)[0:8]
            tile = pltpu.roll(tile, (130 - 4 * iz + 8 * p) % 128, 1)
            total = tile if p == 0 else jnp.where(lanes((8, 128)) // 8 == p, tile, total)
        parts.append(total)
    lane = lanes((24, 128))
    row = rows_of((24, 128)) % 8
    gp, gq, gr = 2 * ix - 2 + lane // 8, 2 * iy - 2 + row, 4 * iz - 2 + lane % 8
    inside = (gp >= 0) & (gp < kx) & (gq >= 0) & (gq < ky) & (gr >= 0) & (gr < kz) & (lane < 48)
    u = jnp.where(inside, jnp.concatenate(parts, 0), 0.0)
    u = around(jnp.where(inside, around(u, 8), 0.0), 8) * BEND
    own = (lane // 16 == 1) & (row // 2 == 1) & ((lane % 8 + 2) // 4 == 1)
    bk_ref[...] = rolled(jnp.where(own, u, 0.0), 80)


def bend(sizes, control, coarse):
    return pl.pallas_call(
        functools.partial(bend_kernel, sizes),
        in_specs=whole(2),
        out_specs=whole(2),
        out_shape=[
            jax.ShapeDtypeStruct((48, 256), f32),
            jax.ShapeDtypeStruct((24, 128), f32),
        ],
        scratch_shapes=[VMEM((48, 256), f32), VMEM((18, 16, 128), f32)],
        cost_estimate=pl.CostEstimate(flops=4000000, bytes_accessed=1000000, transcendentals=0),
        compiler_params=within(8),
        name="bend",
    )(control, coarse)


@functools.cache
def tables():
    own = np.arange(64)
    cross = np.arange(-2, 2)
    wy = np.zeros((24, 64))
    wy[0:12] = weights(own, 12, SPF).T
    wy[16:22] = weights(own, 6, SPC).T
    high, low = halves(wy)
    left = np.concatenate(
        [np.concatenate([high, high], 1), np.concatenate([low, np.zeros_like(low)], 1)], 0
    )
    wc = np.zeros((8, 8, 128), np.float32)
    for j in range(4):
        wc[j, :, :] = weights(cross, 12, SPF)[j, 0:8, None]
        wc[4 + j, 0:6, :] = weights(cross, 6, SPC)[j, :, None]
    fine_scale = SPF**-1.5 / 24.0
    coarse_scale = SPC**-1.5 / 24.0
    wz = np.zeros((2, 128, 128))
    wz[0, :, 0:20] = weights(np.arange(128), 20, SPF) * fine_scale
    wz[1, :, 0:8] = weights(np.arange(128), 8, SPC) * coarse_scale
    wz_high, wz_low = halves(wz)
    m = np.zeros((4, 128, 384))
    fx, cx = weights(own, 12, SPF), weights(own, 6, SPC)
    fz = weights(cross, 20, SPF) * fine_scale
    cz = weights(cross, 8, SPC) * coarse_scale
    fz = np.concatenate([fz, weights(np.arange(126, 128), 20, SPF) * fine_scale])
    cz = np.concatenate([cz, weights(np.arange(126, 128), 8, SPC) * coarse_scale])
    for x in range(64):
        for j in range(6):
            line = m[x // 32 + 2 * (j // 4), 4 * (x % 32) + j % 4]
            for p in range(12):
                at = 128 * (p // 6) + 20 * (p % 6)
                line[at : at + 20] = fx[x, p] * fz[j]
            for p in range(6):
                at = 256 + 80 + 8 * p
                line[at : at + 8] = cx[x, p] * cz[j]
    m_high, m_low = halves(m)
    return left, wc, wz_high, wz_low, m_high, m_low


def along(left, force):
    high, low = split(force)
    both = mm(left, jnp.concatenate([high, low], 0))
    return both[0:24] + both[24:48]


def interior_kernel(s_ref, t_ref, d_ref, left_ref, af_ref, ac_ref, tf_ref, tc_ref):
    fx = weights(np.arange(8), 5, SPF)
    cx = weights(np.arange(64), 6, SPC)
    left = left_ref[...]

    def force(x):
        d = d_ref[x]
        f0 = (s_ref[x, 8:72, :] - s_ref[x + 4, 8:72, :]) + (t_ref[x + 3, 8:72, :] - t_ref[x + 1, 8:72, :])
        s, t = s_ref.at[x + 2], t_ref.at[x + 2]
        f1 = (s[6:70, :] - s[10:74, :]) + (t[9:73, :] - t[7:71, :])
        s, t = s[8:72, :], t[8:72, :]
        f2 = (rolled(s, 2) - rolled(s, 126)) + (rolled(t, 127) - rolled(t, 1))
        return [f0 * d, f1 * d, f2 * d]

    def layers(b):
        for i in range(0, 8, 2):
            section = along(left, jnp.concatenate(force(8 * b + i) + force(8 * b + i + 1), 1))
            for k in range(6):
                at, a = 8 * b + i + k // 3, k % 3
                cols = slice(128 * k, 128 * k + 128)
                tf_ref[at, 16 * a : 16 * a + 16, :] = section[0:16, cols]
                tc_ref[at, 8 * a : 8 * a + 8, :] = section[16:24, cols]

    def block(b):
        for k in range(5):
            total = af_ref[b + k]
            for r in range(8):
                weight = float(fx[r, k])
                if weight != 0.0:
                    total = total + weight * tf_ref[8 * b + r]
            af_ref[b + k] = total
        for k in range((b + 2) // 4, (b + 2) // 4 + 4):
            total = ac_ref[k]
            for r in range(8):
                total = total + float(cx[8 * b + r, k]) * tc_ref[8 * b + r]
            ac_ref[k] = total

    af_ref[...] = jnp.zeros_like(af_ref)
    ac_ref[...] = jnp.zeros_like(ac_ref)
    for b in range(8):
        layers(b)
        if b > 0:
            block(b - 1)
    block(7)


def interior(s, s8, d):
    left = tables()[0]
    return pl.pallas_call(
        interior_kernel,
        in_specs=whole(4),
        out_specs=whole(2),
        out_shape=[
            jax.ShapeDtypeStruct((12, 48, 128), f32),
            jax.ShapeDtypeStruct((6, 24, 128), f32),
        ],
        scratch_shapes=[VMEM((64, 48, 128), f32), VMEM((64, 24, 128), f32)],
        cost_estimate=pl.CostEstimate(flops=40000000, bytes_accessed=4000000, transcendentals=0),
        compiler_params=within(16),
        name="interior",
    )(s, s8, d, jnp.asarray(left))


def crossing(first, second):
    sm2, sm1, dm2, dm1 = (first[i] for i in range(4))
    s0, s1, d0, d1 = (second[i] for i in range(4))
    return [-s0 * dm2, (8.0 * s0 - s1) * dm1, (sm2 - 8.0 * sm1) * d0, sm1 * d1]


def finish_kernel(
    af_ref, ac_ref, xr_ref, xo_ref, yr_ref, yo_ref, zr_ref, zo_ref, bf_ref, bk_ref, left_ref, wc_ref, wzh_ref, wzl_ref, mh_ref, ml_ref,
    chunk_ref, fine_ref, sf_ref, sc_ref,
):
    n = chunk_ref.shape[0]
    edge_f = weights(np.arange(-2, 2), 4, SPF)
    edge_c = weights(np.arange(-2, 2), 4, SPC)
    left = left_ref[...]
    lane = lanes((64, 128))

    edge = along(left, jnp.concatenate(crossing(xr_ref, xo_ref), 1))
    sf_ref[...] = af_ref[...]
    sc_ref[...] = ac_ref[...]
    for k in range(4):
        for j in range(4):
            cols = slice(128 * j, 128 * j + 128)
            fine = float(edge_f[j, k]) * edge[0:16, cols]
            coarse = float(edge_c[j, k]) * edge[16:24, cols]
            total_f = fine if j == 0 else total_f + fine
            total_c = coarse if j == 0 else total_c + coarse
        sf_ref[k, 0:16, :] += total_f
        sc_ref[k, 0:8, :] += total_c

    edge = along(left, jnp.concatenate(crossing(yr_ref, yo_ref), 1))
    for p in range(12):
        total = sf_ref[p, 16:24, :]
        for j in range(4):
            total = total + wc_ref[j] * edge[p : p + 1, 128 * j : 128 * j + 128]
        sf_ref[p, 16:24, :] = total
    for p in range(6):
        total = sc_ref[p, 8:16, :]
        for j in range(4):
            total = total + wc_ref[4 + j] * edge[16 + p : 17 + p, 128 * j : 128 * j + 128]
        sc_ref[p, 8:16, :] = total

    zf = mm3(sf_ref[...].reshape(576, 128), wzh_ref[0], wzl_ref[0])
    zc = mm3(sc_ref[...].reshape(144, 128), wzh_ref[1], wzl_ref[1])
    fine = []
    for h in range(2):
        total = zf[288 * h : 288 * h + 48]
        for i in range(1, 6):
            total = total + rolled(zf[48 * (6 * h + i) : 48 * (6 * h + i) + 48], 20 * i)
        fine.append(total + bf_ref[:, 128 * h : 128 * h + 128])
    coarse = bk_ref[...] + rolled(zc[0:24], 80)
    for p in range(1, 6):
        coarse = coarse + rolled(zc[24 * p : 24 * p + 24], 80 + 8 * p)

    j = lane % 4
    extra = None
    for h in range(2):
        s = jnp.where(j < 2, rolled(zr_ref[0], -2 * h) - zo_ref[h], zo_ref[h])
        d = jnp.where(j < 2, rolled(zr_ref[1], -2 * h), zo_ref[2 + h])
        slope = jnp.where(j >= 2, rolled(s, 2), 0.0) - jnp.where(j < 2, rolled(s, 126), 0.0)
        slope = slope + 8.0 * (
            jnp.where(j == 1, rolled(s, 127), 0.0) - jnp.where(j == 2, rolled(s, 1), 0.0)
        )
        wrapped = jnp.where(j < 2, -slope * zo_ref[2 + h], 0.0)
        part = along(left, jnp.concatenate([slope * d, wrapped], 1))
        part = mm3(part[:, 0:128], mh_ref[h], ml_ref[h]) + mm3(part[:, 128:256], mh_ref[2 + h], ml_ref[2 + h])
        extra = part if extra is None else extra + part

    zero8 = jnp.zeros((8, 128), f32)
    zero32 = jnp.zeros((32, 128), f32)
    low = fine[0] + jnp.concatenate([zero32, extra[0:16, 0:128]], 0)
    high = fine[1] + jnp.concatenate([zero32, extra[0:16, 128:256]], 0)
    spread = jnp.concatenate(
        [coarse[0:8], zero8, coarse[8:16], zero8, coarse[16:24] + extra[16:24, 256:384], zero8], 0
    )
    fine_ref[:, 0:128] = low
    fine_ref[:, 128:256] = high
    lane = lanes((48, 128))
    chunk = jnp.where(lane < 40, low, jnp.where(lane < 80, rolled(high, 88), spread))
    for i in range(n):
        for a in range(3):
            chunk_ref[i, 12 * a : 12 * a + 12, :] = chunk[16 * a : 16 * a + 12]
        chunk_ref[i, 36:40, :] = zero8[0:4]


def finish(n, *values):
    constants = tables()
    return pl.pallas_call(
        finish_kernel,
        in_specs=whole(16),
        out_specs=whole(2),
        out_shape=[
            jax.ShapeDtypeStruct((n, 40, 128), f32),
            jax.ShapeDtypeStruct((48, 256), f32),
        ],
        scratch_shapes=[VMEM((12, 48, 128), f32), VMEM((6, 24, 128), f32)],
        compiler_params=within(12),
        name="finish",
    )(*values, *(jnp.asarray(c) for c in constants))


def sides(ref, axis):
    n = ref.shape[0]
    i = lax.axis_index(axis)
    return ref[jnp.maximum(i - 1, 0)], i > 0, ref[jnp.minimum(i + 1, n - 1)], i < n - 1


def x_kernel(ny, got_ref, fine_ref, chunk_ref, own_ref, pack_ref):
    n = got_ref.shape[0]
    lane = lanes((24, 128))
    coarse = jnp.zeros((24, 128), f32)
    for j in range(n):
        part = jnp.concatenate([got_ref[j, 12 * a : 12 * a + 8, :] for a in range(3)], 0)
        first, last = max(0, 16 * j - 16), min(16 * n, 16 * j + 32)
        coarse = coarse + jnp.where((lane >= first) & (lane < last), rolled(part, 16 * j - 96), 0.0)
    low, has_low, high, has_high = sides(got_ref, "gx")
    lane = lanes((12, 128))
    middle = (lane >= 40) & (lane < 80)
    own_ref[...] = fine_ref[...]
    for a in range(3):
        rows = slice(16 * a, 16 * a + 12)
        own_ref[rows, 0:128] += jnp.where(middle & has_low, low[12 * a : 12 * a + 12], 0.0)
        own_ref[rows, 128:256] += jnp.where(middle & has_high, rolled(high[12 * a : 12 * a + 12], 40), 0.0)
    pack_ref[0:24, :] = coarse
    lane = lanes((2, 128))
    for m, q in ((0, 0), (2, 10)):
        last = jnp.zeros((2, 128), f32)
        for a in range(3):
            first = own_ref[16 * a + q : 16 * a + q + 2, 0:128]
            second = own_ref[16 * a + q : 16 * a + q + 2, 128:256]
            pack_ref[24 + 4 * a + m : 26 + 4 * a + m, :] = jnp.where(lane < 40, second, first)
            last = jnp.where((lane >= 40 * a) & (lane < 40 * a + 40), rolled(second, 40 * a - 40), last)
        pack_ref[36 + m : 38 + m, :] = last
    for i in range(ny):
        chunk_ref[i] = pack_ref[...]


def x_stage(ny, got, fine):
    return pl.pallas_call(
        functools.partial(x_kernel, ny),
        in_specs=whole(2),
        out_specs=whole(2),
        out_shape=[
            jax.ShapeDtypeStruct((ny, 40, 128), f32),
            jax.ShapeDtypeStruct((48, 256), f32),
        ],
        scratch_shapes=[VMEM((40, 128), f32)],
        compiler_params=within(4),
        name="xstage",
    )(got, fine)


def lane_of(p):
    return 128 * (p // 6), 20 * (p % 6)


def y_kernel(nz, got_ref, fine_ref, chunk_ref, own_ref, sum_ref):
    n = got_ref.shape[0]
    sum_ref[...] = jnp.zeros_like(sum_ref)
    for j in range(n):
        for a in range(3):
            at = 24 * a + 2 * j
            sum_ref[at : at + 6, :] += got_ref[j, 8 * a : 8 * a + 6, :]
    low, has_low, high, has_high = sides(got_ref, "gy")
    own_ref[...] = fine_ref[...]
    lane = lanes((2, 128))
    inner, tail = lane < 40, (lane >= 40) & (lane < 80)
    for a in range(3):
        for got, valid, m, q in ((low, has_low, 2, 2), (high, has_high, 0, 8)):
            rows = slice(16 * a + q, 16 * a + q + 2)
            first = got[24 + 4 * a + m : 26 + 4 * a + m]
            last = rolled(got[36 + m : 38 + m], 40 - 40 * a)
            second = jnp.where(inner, first, jnp.where(tail, last, 0.0))
            own_ref[rows, 0:128] += jnp.where(valid & ~inner, first, 0.0)
            own_ref[rows, 128:256] += jnp.where(valid, second, 0.0)
    lane = lanes((8, 128))
    border = jnp.zeros((8, 128), f32)
    for a in range(3):
        for p in range(8):
            tile, base = lane_of(p + 2)
            v = own_ref[16 * a + 2 : 16 * a + 10, tile : tile + 128]
            at = 32 * a + 4 * p
            border = jnp.where((lane >= at) & (lane < at + 2), rolled(v, at - base), border)
            border = jnp.where((lane >= at + 2) & (lane < at + 4), rolled(v, at - base - 16), border)
    for i in range(nz):
        for a in range(3):
            chunk_ref[i, 16 * a : 16 * a + 16, :] = sum_ref[24 * a + 2 : 24 * a + 18, :]
        chunk_ref[i, 48:56, :] = border


def y_stage(nz, got, fine):
    return pl.pallas_call(
        functools.partial(y_kernel, nz),
        in_specs=whole(2),
        out_specs=whole(2),
        out_shape=[
            jax.ShapeDtypeStruct((nz, 56, 128), f32),
            jax.ShapeDtypeStruct((48, 256), f32),
        ],
        scratch_shapes=[VMEM((72, 128), f32)],
        compiler_params=within(4),
        name="ystage",
    )(got, fine)


def z_kernel(nx, ny, got_ref, fine_ref, out_fine_ref, out_coarse_ref):
    n = got_ref.shape[0]
    low, has_low, high, has_high = sides(got_ref, "gz")
    low = jnp.where(has_low, low[48:56], 0.0)
    high = jnp.where(has_high, high[48:56], 0.0)
    lane = lanes((8, 128))
    for a in range(3):
        for p in range(8):
            tile, base = lane_of(p + 2)
            v = fine_ref[16 * a + 2 : 16 * a + 10, tile : tile + 128]
            at = 32 * a + 4 * p
            v = v + jnp.where((lane >= base + 2) & (lane < base + 4), rolled(low, base - at), 0.0)
            v = v + jnp.where((lane >= base + 16) & (lane < base + 18), rolled(high, base + 16 - at), 0.0)
            out_fine_ref[a, p] = rolled(v, -(base + 2))[:, 0:16]

    lane = lanes((48, 128))
    k = lane % 8
    parts = [got_ref[m, 0:48, :] for m in range(n)]
    tiles = []
    for m in range(0, n, 2):
        total = jnp.where(k < 6, rolled(parts[m], -2), 0.0) + jnp.where(k >= 2, rolled(parts[m + 1], 2), 0.0)
        if m > 0:
            total = total + jnp.where(k < 2, rolled(parts[m - 1], -6), 0.0)
        if m + 2 < n:
            total = total + jnp.where(k >= 6, rolled(parts[m + 2], 6), 0.0)
        tiles.append(total)
    per = len(tiles)
    slot = lane // 8 % per
    for h in range(per):
        total = rolled(tiles[0], -8 * h)
        for m in range(1, per):
            total = jnp.where(slot == m, rolled(tiles[m], 8 * (m - h)), total)
        for g in range(2 * nx // per):
            points = rolled(total, -8 * per * g)
            for a in range(3):
                out_coarse_ref[a, per * g + h] = points[16 * a : 16 * a + 2 * ny, 0 : 4 * n]


def z_stage(sizes, got, fine):
    nx, ny, nz = sizes
    return pl.pallas_call(
        functools.partial(z_kernel, nx, ny),
        in_specs=whole(2),
        out_specs=whole(2),
        out_shape=[
            jax.ShapeDtypeStruct((3, 8, 8, 16), f32),
            jax.ShapeDtypeStruct((3, 2 * nx, 2 * ny, 4 * nz), f32),
        ],
        compiler_params=within(6),
        name="zstage",
    )(got, fine)


def shifted_up(values, axis):
    return lax.ppermute(values, axis, [(i, i + 1) for i in range(lax.axis_size(axis) - 1)])


def exchanged(chunks, axis):
    return lax.all_to_all(chunks, axis, split_axis=0, concat_axis=0, tiled=True)


def per_device(warped_image, fixed_image, fine_control, coarse_control):
    sizes = tuple(lax.axis_size(n) for n in ("gx", "gy", "gz"))
    xf, xo, yf, yo, zf, zo, s, s8, d = faces(warped_image, fixed_image)
    yr = shifted_up(yf, "gy")
    zr = shifted_up(zf, "gz")
    xr = shifted_up(xf, "gx")
    bent_fine, bent_coarse = bend(sizes, fine_control, coarse_control)
    fine, coarse = interior(s, s8, d)
    chunk, fine = finish(sizes[0], fine, coarse, xr, xo, yr, yo, zr, zo, bent_fine, bent_coarse)
    chunk, fine = x_stage(sizes[1], exchanged(chunk, "gx"), fine)
    chunk, fine = y_stage(sizes[2], exchanged(chunk, "gy"), fine)
    return tuple(z_stage(sizes, exchanged(chunk, "gz"), fine))


def solution(mesh):
    in_specs = (P("gx", "gy", "gz"), P("gx", "gy", "gz"), P(None, "gx", "gy", "gz"), P())
    out_specs = (P(None, "gx", "gy", "gz"), P())
    return jax.shard_map(
        per_device, mesh=mesh, in_specs=in_specs, out_specs=out_specs, check_vma=False
    )
```

profile of v0, /device:TPU:2, one launch (start us, length us, event | category | flops | bytes accessed | tf_op | source)
XLA Modules:
  0.0 65.1 jit_solution(9850252984722124338)
XLA Ops:
  0.6 0.0 copy-start.6
  0.6 0.0 copy-start.3
  0.7 0.0 copy-start.2
  0.7 2.9 %faces.1 = (f32[4,64,128]{2,1,0:T(8,128)S(1)}, f32[4,64,128]{2,1,0:T(8,128)S(1)}, f32[4,64,128]{2,1,0:T(8,128)S(1)}, f32[4,64,128]{2,1,0:T(8,128)S(1)}, f32[2,64...) custom-call(f32[64,64,128]{2,1,0:T(8,128)} %w_hbm.1, ...), custom_call_target="tpu_custom_call" | custom-call | tf_op jit(solution)/shard_map/faces/pallas_call | solution.py:127
  3.5 1.9 %collective-permute-start = (f32[4,64,128]{2,1,0:T(8,128)S(1)}, f32[4,64,128]{2,1,0:T(8,128)S(1)}, u32[]{:S(2)}, u32[]{:S(2)}) collective-permute-start(f32[4,64,128]{2,1,0:T(8,128)S(1)} %get-tuple-element.26), channel_id=1, source_target_pairs={{0,64},{64,128},{128,192},{192,256},{256,320},{320,384},{384,448},... | collective-permute-start | bytes 393224 | tf_op jit(solution)/shard_map/ppermute | solution.py:574
  5.5 3.5 %collective-permute-start.1 = (f32[4,64,128]{2,1,0:T(8,128)S(1)}, f32[4,64,128]{2,1,0:T(8,128)S(1)}, u32[]{:S(2)}, u32[]{:S(2)}) collective-permute-start(f32[4,64,128]{2,1,0:T(8,128)S(1)} %get-tuple-element.28), channel_id=1, source_target_pairs={{0,8},{8,16},{16,24},{24,32},{32,40},{40,48},{48,56},{1,9},{9,17},... | collective-permute-start | bytes 393224 | tf_op jit(solution)/shard_map/ppermute | solution.py:574
  9.0 4.3 %collective-permute-start.2 = (f32[2,64,128]{2,1,0:T(8,128)S(1)}, f32[2,64,128]{2,1,0:T(8,128)S(1)}, u32[]{:S(2)}, u32[]{:S(2)}) collective-permute-start(f32[2,64,128]{2,1,0:T(8,128)S(1)} %get-tuple-element.30), channel_id=1, source_target_pairs={{0,1},{1,2},{2,3},{3,4},{4,5},{5,6},{6,7},{8,9},{9,10},{10,11},{11... | collective-permute-start | bytes 196616 | tf_op jit(solution)/shard_map/ppermute | solution.py:574
  13.3 0.0 copy-done.3
  13.3 0.0 copy-done.2
  13.3 0.4 bend.1
  13.7 0.0 copy-done.6
  13.7 0.0 copy-start
  13.7 0.0 copy-start.1
  13.7 0.0 copy-start.4
  13.8 0.0 copy-start.5
  13.8 0.0 copy-start.7
  13.8 2.9 %interior.1 = (f32[12,48,128]{2,1,0:T(8,128)S(1)}, f32[6,24,128]{2,1,0:T(8,128)S(1)}) custom-call(f32[68,80,128]{2,1,0:T(8,128)S(1)} %get-tuple-element.21.s_ref, f32[68,80,128]{2,1,0:T(8,128)S(1)} %get-tuple-element.22.t_ref, f32[64,64,128]{2,1,0:T(8,128)S(1)} %get-tuple-element.23.d_ref, bf16[48,128]{1,0:T(8,128)(2,1)S(1)} %copy-done.6), custom_call_target="tpu_custom_call" | custom-call | flops 40000000 | bytes 4000000 | tf_op jit(solution)/shard_map/interior/pallas_call | solution.py:301
  16.7 0.0 collective-permute-done.2.zr_ref
  16.7 0.0 collective-permute-done.xr_ref
  16.7 0.0 collective-permute-done.1.yr_ref
  16.8 0.0 copy-done
  16.8 0.0 copy-done.1
  16.8 0.0 copy-done.4
  16.8 0.0 copy-done.5
  16.8 0.0 copy-done.7
  16.8 0.9 %finish.1 = (f32[8,40,128]{2,1,0:T(8,128)S(1)}, f32[48,256]{1,0:T(8,128)S(1)}) custom-call(f32[12,48,128]{2,1,0:T(8,128)S(1)} %get-tuple-element.24.af_ref, f32[6,24,128]{2,1,0:T(8,128)S(1)} %get-tuple-element.25.ac_ref, f32[4,64,128]{2,1,0:T(8,128)S(1)} %collective-permute-done.xr_ref, f32[4,64,128]{2,1,0:T(8,128)S(1)} %get-tuple-element.27.xo_ref, ...), custom_call_target="tpu_custom_call" | custom-call | tf_op jit(solution)/shard_map/finish/pallas_call | solution.py:402
  17.7 10.0 %all_to_all.15.got_ref = f32[8,40,128]{2,1,0:T(8,128)S(1)} all-to-all(f32[8,40,128]{2,1,0:T(8,128)S(1)} %get-tuple-element.34), channel_id=1, replica_groups=mesh['gx'=8,'gy'=8,'gz'=8] {'gx'}, dimensions={0} | all-to-all | bytes 327680 | tf_op jit(solution)/shard_map/all_to_all | solution.py:578
  27.7 0.2 xstage.1
  27.9 15.5 %all_to_all.16.got_ref = f32[8,40,128]{2,1,0:T(8,128)S(1)} all-to-all(f32[8,40,128]{2,1,0:T(8,128)S(1)} %get-tuple-element.36), channel_id=1, replica_groups=mesh['gx'=8,'gy'=8,'gz'=8] {'gy'}, dimensions={0} | all-to-all | bytes 327680 | tf_op jit(solution)/shard_map/all_to_all | solution.py:578
  43.4 0.2 ystage.1
  43.6 20.1 %all_to_all.17.got_ref = f32[8,56,128]{2,1,0:T(8,128)S(1)} all-to-all(f32[8,56,128]{2,1,0:T(8,128)S(1)} %get-tuple-element.38), channel_id=1, replica_groups=mesh['gx'=8,'gy'=8,'gz'=8] {'gz'}, dimensions={0} | all-to-all | bytes 458752 | tf_op jit(solution)/shard_map/all_to_all | solution.py:578
  63.7 1.4 %zstage.1 = (f32[3,8,8,16]{3,2,1,0:T(8,128)}, f32[3,16,16,32]{3,2,1,0:T(8,128)}) custom-call(f32[8,56,128]{2,1,0:T(8,128)S(1)} %all_to_all.17.got_ref, f32[48,256]{1,0:T(8,128)S(1)} %get-tuple-element.39.fine_ref), custom_call_target="tpu_custom_call" | custom-call | tf_op jit(solution)/shard_map/zstage/pallas_call | solution.py:560
Async XLA Ops:
  0.6 13.1 %copy-start.6 = (bf16[48,128]{1,0:T(8,128)(2,1)S(1)}, bf16[48,128]{1,0:T(8,128)(2,1)}, u32[]{:S(2)}) copy-start(bf16[48,128]{1,0:T(8,128)(2,1)} %constant.12.clone.left_ref) | copy-start | bytes 36868
  0.6 12.6 %copy-start.3 = (f32[3,8,8,16]{3,2,1,0:T(8,128)S(1)}, f32[3,8,8,16]{3,2,1,0:T(8,128)}, u32[]{:S(2)}) copy-start(f32[3,8,8,16]{3,2,1,0:T(8,128)} %c_ref.1) | copy-start | bytes 36868
  0.7 12.6 %copy-start.2 = (f32[3,16,16,32]{3,2,1,0:T(8,128)S(1)}, f32[3,16,16,32]{3,2,1,0:T(8,128)}, u32[]{:S(2)}) copy-start(f32[3,16,16,32]{3,2,1,0:T(8,128)} %k_ref.1) | copy-start | bytes 294916
  3.5 13.2 %collective-permute-start = (f32[4,64,128]{2,1,0:T(8,128)S(1)}, f32[4,64,128]{2,1,0:T(8,128)S(1)}, u32[]{:S(2)}, u32[]{:S(2)}) collective-permute-start(f32[4,64,128]{2,1,0:T(8,128)S(1)} %get-tuple-element.26), channel_id=1, source_target_pairs={{0,64},{64,128},{128,192},{192,256},{256,320},{320,384},{384,448},... | collective-permute-start | bytes 393224 | tf_op jit(solution)/shard_map/ppermute | solution.py:574
  5.5 11.3 %collective-permute-start.1 = (f32[4,64,128]{2,1,0:T(8,128)S(1)}, f32[4,64,128]{2,1,0:T(8,128)S(1)}, u32[]{:S(2)}, u32[]{:S(2)}) collective-permute-start(f32[4,64,128]{2,1,0:T(8,128)S(1)} %get-tuple-element.28), channel_id=1, source_target_pairs={{0,8},{8,16},{16,24},{24,32},{32,40},{40,48},{48,56},{1,9},{9,17},... | collective-permute-start | bytes 393224 | tf_op jit(solution)/shard_map/ppermute | solution.py:574
  9.0 7.8 %collective-permute-start.2 = (f32[2,64,128]{2,1,0:T(8,128)S(1)}, f32[2,64,128]{2,1,0:T(8,128)S(1)}, u32[]{:S(2)}, u32[]{:S(2)}) collective-permute-start(f32[2,64,128]{2,1,0:T(8,128)S(1)} %get-tuple-element.30), channel_id=1, source_target_pairs={{0,1},{1,2},{2,3},{3,4},{4,5},{5,6},{6,7},{8,9},{9,10},{10,11},{11... | collective-permute-start | bytes 196616 | tf_op jit(solution)/shard_map/ppermute | solution.py:574
  13.7 3.0 %copy-start = (bf16[4,128,384]{2,1,0:T(8,128)(2,1)S(1)}, bf16[4,128,384]{2,1,0:T(8,128)(2,1)}, u32[]{:S(2)}) copy-start(bf16[4,128,384]{2,1,0:T(8,128)(2,1)} %constant.16.clone.mh_ref) | copy-start | bytes 1179652
  13.7 3.0 %copy-start.1 = (bf16[4,128,384]{2,1,0:T(8,128)(2,1)S(1)}, bf16[4,128,384]{2,1,0:T(8,128)(2,1)}, u32[]{:S(2)}) copy-start(bf16[4,128,384]{2,1,0:T(8,128)(2,1)} %constant.17.clone.ml_ref) | copy-start | bytes 1179652
  13.7 3.0 %copy-start.4 = (bf16[2,128,128]{2,1,0:T(8,128)(2,1)S(1)}, bf16[2,128,128]{2,1,0:T(8,128)(2,1)}, u32[]{:S(2)}) copy-start(bf16[2,128,128]{2,1,0:T(8,128)(2,1)} %constant.14.clone.wzh_ref) | copy-start | bytes 196612
  13.8 3.0 %copy-start.5 = (bf16[2,128,128]{2,1,0:T(8,128)(2,1)S(1)}, bf16[2,128,128]{2,1,0:T(8,128)(2,1)}, u32[]{:S(2)}) copy-start(bf16[2,128,128]{2,1,0:T(8,128)(2,1)} %constant.15.clone.wzl_ref) | copy-start | bytes 196612
  13.8 3.0 %copy-start.7 = (f32[8,8,128]{2,1,0:T(8,128)S(1)}, f32[8,8,128]{2,1,0:T(8,128)}, u32[]{:S(2)}) copy-start(f32[8,8,128]{2,1,0:T(8,128)} %constant.13.clone.wc_ref) | copy-start | bytes 98308
where the time goes:
time: 65.4 us; the launch traced here: 65.1 us
  blocking collectives  45.6 us (70%)
  starting transfers between devices  9.69 us (15%)
  Pallas kernels  8.91 us (14%)
  between operations  0.83 us (1%)
    all_to_all x3, blocking collectives, exchanged(): return lax.all_to_all(chunks, axis, split_axis=0, concat_axis=0, tiled=True)  45.6 us
    ppermute x3, starting transfers between devices, shifted_up(): lax.ppermute(values, axis, [(i, i + 1) for i in range(lax.axis_size(axis)...  9.69 us
    pallas_call x1, Pallas kernels, interior(): pl.pallas_call(interior_kernel, in_specs=whole(4), out_specs=whole(2), ou...  2.94 us
    pallas_call x1, Pallas kernels, faces(): pl.pallas_call(faces_kernel, in_specs=[pl.BlockSpec(memory_space=pltpu.HB...  2.87 us
    pallas_call x1, Pallas kernels, z_stage(): pl.pallas_call(functools.partial(z_kernel, nx, ny), in_specs=whole(2), ou...  1.38 us
  transfers between devices with their start and end apart: 3, of which 0 were waited for; matrix products, arithmetic and copies ran while one was open for 0% of the time, Pallas kernels for 5%

commit v1 on v0

--- a/solution.py
+++ b/solution.py
@@ -69,20 +69,43 @@
     return [pl.BlockSpec(memory_space=VMEM)] * n
 
 
-PARTS = ((0, 4), (4, 12), (16, 16), (32, 16), (48, 16))
-
-
-def faces_kernel(w_hbm, f_hbm, xf_ref, xo_ref, yf_ref, yo_ref, zf_ref, zo_ref, s_ref, t_ref, d_ref, w_ref, f_ref, sem):
-    def copies(g):
-        part = pl.ds(*PARTS[g])
-        return [
-            pltpu.make_async_copy(hbm.at[part], ref.at[part], sem.at[i, g])
-            for i, (hbm, ref) in enumerate(((w_hbm, w_ref), (f_hbm, f_ref)))
-        ]
-
-    for g in range(len(PARTS)):
-        for copy in copies(g):
-            copy.start()
+def edges_kernel(w_hbm, f_hbm, xf_ref, yf_ref, px_ref, py_ref, sem):
+    copies = []
+    for i, hbm in enumerate((w_hbm, f_hbm)):
+        copies.append(pltpu.make_async_copy(hbm.at[:, pl.ds(56, 8)], py_ref.at[i], sem.at[0, i]))
+        copies.append(pltpu.make_async_copy(hbm.at[pl.ds(62, 2)], px_ref.at[i], sem.at[1, i]))
+    for copy in copies:
+        copy.start()
+    for copy in copies:
+        copy.wait()
+    for x in range(64):
+        w, f = py_ref[0, x], py_ref[1, x]
+        s, d = w + f, w - f
+        for j in range(2):
+            yf_ref[j, x : x + 1, :] = s[6 + j : 7 + j]
+            yf_ref[2 + j, x : x + 1, :] = d[6 + j : 7 + j]
+    xf_ref[0:2] = px_ref[0] + px_ref[1]
+    xf_ref[2:4] = px_ref[0] - px_ref[1]
+
+
+def edges(w, f):
+    return pl.pallas_call(
+        edges_kernel,
+        in_specs=[pl.BlockSpec(memory_space=pltpu.HBM)] * 2,
+        out_specs=whole(2),
+        out_shape=[jax.ShapeDtypeStruct((4, 64, 128), f32)] * 2,
+        scratch_shapes=[
+            VMEM((2, 2, 64, 128), f32),
+            VMEM((2, 64, 8, 128), f32),
+            pltpu.SemaphoreType.DMA((2, 2)),
+        ],
+        cost_estimate=pl.CostEstimate(flops=1000000, bytes_accessed=1000000, transcendentals=0),
+        compiler_params=within(4),
+        name="edges",
+    )(*(pltpu.with_memory_space_constraint(v, pltpu.HBM) for v in (w, f)))
+
+
+def faces_kernel(w_ref, f_ref, xo_ref, yo_ref, zf_ref, zo_ref, s_ref, t_ref, d_ref):
     lane = lanes((64, 128))
     for ref in (s_ref, t_ref):
         ref[:, 0:8, :] = jnp.zeros((68, 8, 128), f32)
@@ -90,53 +113,42 @@
         for x in (0, 1, 66, 67):
             ref[x, 8:72, :] = jnp.zeros((64, 128), f32)
 
-    for g, (start, size) in enumerate(PARTS):
-        for copy in copies(g):
-            copy.wait()
-        for x in range(start, start + size):
-            w = w_ref[x]
-            f = f_ref[x]
-            s = w + f
-            d = w - f
-            s_ref[x + 2, 8:72, :] = s
-            t_ref[x + 2, 8:72, :] = 8.0 * s
-            d_ref[x] = d
-            for j in range(2):
-                yf_ref[j, x : x + 1, :] = s[62 + j : 63 + j]
-                yf_ref[2 + j, x : x + 1, :] = d[62 + j : 63 + j]
-                yo_ref[j, x : x + 1, :] = s[j : j + 1]
-                yo_ref[2 + j, x : x + 1, :] = d[j : j + 1]
-            i = x % 32
-            here = (lane >= 4 * i) & (lane < 4 * i + 4)
-            packed_s = rolled(s, 4 * i + 2) if i == 0 else jnp.where(here, rolled(s, 4 * i + 2), packed_s)
-            packed_d = rolled(d, 4 * i + 2) if i == 0 else jnp.where(here, rolled(d, 4 * i + 2), packed_d)
-            if i == 31:
-                zo_ref[x // 32] = packed_s
-                zo_ref[2 + x // 32] = packed_d
+    for x in range(64):
+        w = w_ref[x]
+        f = f_ref[x]
+        s = w + f
+        d = w - f
+        s_ref[x + 2, 8:72, :] = s
+        t_ref[x + 2, 8:72, :] = 8.0 * s
+        d_ref[x] = d
+        for j in range(2):
+            yo_ref[j, x : x + 1, :] = s[j : j + 1]
+            yo_ref[2 + j, x : x + 1, :] = d[j : j + 1]
+        i = x % 32
+        here = (lane >= 4 * i) & (lane < 4 * i + 4)
+        packed_s = rolled(s, 4 * i + 2) if i == 0 else jnp.where(here, rolled(s, 4 * i + 2), packed_s)
+        packed_d = rolled(d, 4 * i + 2) if i == 0 else jnp.where(here, rolled(d, 4 * i + 2), packed_d)
+        if i == 31:
+            zo_ref[x // 32] = packed_s
+            zo_ref[2 + x // 32] = packed_d
 
     for j in range(2):
-        xf_ref[j] = s_ref[64 + j, 8:72, :]
-        xf_ref[2 + j] = d_ref[62 + j]
         xo_ref[j] = s_ref[2 + j, 8:72, :]
         xo_ref[2 + j] = d_ref[j]
         zf_ref[j] = jnp.where(lane % 4 < 2, zo_ref[2 * j], rolled(zo_ref[2 * j + 1], 2))
 
 
 def faces(w, f):
-    shapes = [(4, 64, 128)] * 4 + [(2, 64, 128), (4, 64, 128)] + [(68, 80, 128)] * 2 + [(64, 64, 128)]
+    shapes = [(4, 64, 128)] * 2 + [(2, 64, 128), (4, 64, 128)] + [(68, 80, 128)] * 2 + [(64, 64, 128)]
     return pl.pallas_call(
         faces_kernel,
-        in_specs=[pl.BlockSpec(memory_space=pltpu.HBM)] * 2,
-        out_specs=whole(9),
+        in_specs=whole(2),
+        out_specs=whole(7),
         out_shape=[jax.ShapeDtypeStruct(s, f32) for s in shapes],
-        scratch_shapes=[
-            VMEM((64, 64, 128), f32),
-            VMEM((64, 64, 128), f32),
-            pltpu.SemaphoreType.DMA((2, len(PARTS))),
-        ],
-        compiler_params=within(16),
+        cost_estimate=pl.CostEstimate(flops=20000000, bytes_accessed=4000000, transcendentals=0),
+        compiler_params=within(4),
         name="faces",
-    )(*(pltpu.with_memory_space_constraint(v, pltpu.HBM) for v in (w, f)))
+    )(w, f)
 
 
 def bend_kernel(sizes, c_ref, k_ref, bf_ref, bk_ref, u_ref, k2_ref):
@@ -580,10 +592,11 @@
 
 def per_device(warped_image, fixed_image, fine_control, coarse_control):
     sizes = tuple(lax.axis_size(n) for n in ("gx", "gy", "gz"))
-    xf, xo, yf, yo, zf, zo, s, s8, d = faces(warped_image, fixed_image)
+    xf, yf = edges(warped_image, fixed_image)
     yr = shifted_up(yf, "gy")
+    xr = shifted_up(xf, "gx")
+    xo, yo, zf, zo, s, s8, d = faces(warped_image, fixed_image)
     zr = shifted_up(zf, "gz")
-    xr = shifted_up(xf, "gx")
     bent_fine, bent_coarse = bend(sizes, fine_control, coarse_control)
     fine, coarse = interior(s, s8, d)
     chunk, fine = finish(sizes[0], fine, coarse, xr, xo, yr, yo, zr, zo, bent_fine, bent_coarse)

time: 65.4 us -> 65.4 us (level)
    pallas_call x1 -> x2, Pallas kernels: 2.87 us -> 2.64 us  [the longest x1 1.33 us: edges(): pl.pallas_call(edges_kernel, in_specs=[pl.BlockSpec(memory_space=pltpu.HB...]
  transfers between devices with their start and end apart: 3 -> 3, of which waited for: 0 -> 0; matrix products, arithmetic and copies ran while one was open for 0% -> 0% of each run, Pallas kernels for 5% -> 8%
where the time goes in v1:
time: 65.4 us; the launch traced here: 65.2 us
  blocking collectives  45.2 us (69%)
  starting transfers between devices  9.95 us (15%)
  Pallas kernels  9.03 us (14%)
  between operations  0.87 us (1%)
    all_to_all x3, blocking collectives, exchanged(): return lax.all_to_all(chunks, axis, split_axis=0, concat_axis=0, tiled=True)  45.2 us
    ppermute x3, starting transfers between devices, shifted_up(): lax.ppermute(values, axis, [(i, i + 1) for i in range(lax.axis_size(axis)...  9.95 us
    pallas_call x1, Pallas kernels, interior(): pl.pallas_call(interior_kernel, in_specs=whole(4), out_specs=whole(2), ou...  3.29 us
    pallas_call x1, Pallas kernels, z_stage(): pl.pallas_call(functools.partial(z_kernel, nx, ny), in_specs=whole(2), ou...  1.38 us
    pallas_call x1, Pallas kernels, edges(): pl.pallas_call(edges_kernel, in_specs=[pl.BlockSpec(memory_space=pltpu.HB...  1.33 us
  transfers between devices with their start and end apart: 3, of which 0 were waited for; matrix products, arithmetic and copies ran while one was open for 0% of the time, Pallas kernels for 8%

profile of v1, /device:TPU:2, one launch (start us, length us, event | category | flops | bytes accessed | tf_op | source)
XLA Modules:
  0.0 65.2 jit_solution(13332554955799263247)
XLA Ops:
  0.6 0.0 copy-start
  0.6 0.0 copy-start.1
  0.6 1.3 %edges.1 = (f32[4,64,128]{2,1,0:T(8,128)S(1)}, f32[4,64,128]{2,1,0:T(8,128)S(1)}) custom-call(f32[64,64,128]{2,1,0:T(8,128)} %w_hbm.1, f32[64,64,128]{2,1,0:T(8,128)} %f_hbm.1), custom_call_target="tpu_custom_call" | custom-call | flops 1000000 | bytes 1000000 | tf_op jit(solution)/shard_map/edges/pallas_call | solution.py:92
  2.0 2.1 %collective-permute-start = (f32[4,64,128]{2,1,0:T(8,128)S(1)}, f32[4,64,128]{2,1,0:T(8,128)S(1)}, u32[]{:S(2)}, u32[]{:S(2)}) collective-permute-start(f32[4,64,128]{2,1,0:T(8,128)S(1)} %get-tuple-element.26), channel_id=1, source_target_pairs={{0,64},{64,128},{128,192},{192,256},{256,320},{320,384},{384,448},... | collective-permute-start | bytes 393224 | tf_op jit(solution)/shard_map/ppermute | solution.py:586
  4.0 0.0 copy-start.4
  4.1 0.0 copy-start.5
  4.1 0.0 copy-start.8
  4.1 3.6 %collective-permute-start.1 = (f32[4,64,128]{2,1,0:T(8,128)S(1)}, f32[4,64,128]{2,1,0:T(8,128)S(1)}, u32[]{:S(2)}, u32[]{:S(2)}) collective-permute-start(f32[4,64,128]{2,1,0:T(8,128)S(1)} %get-tuple-element.28), channel_id=1, source_target_pairs={{0,8},{8,16},{16,24},{24,32},{32,40},{40,48},{48,56},{1,9},{9,17},... | collective-permute-start | bytes 393224 | tf_op jit(solution)/shard_map/ppermute | solution.py:586
  7.7 0.0 copy-done
  7.7 0.0 copy-done.1
  7.7 1.3 %faces.1 = (f32[4,64,128]{2,1,0:T(8,128)S(1)}, f32[4,64,128]{2,1,0:T(8,128)S(1)}, f32[2,64,128]{2,1,0:T(8,128)S(1)}, f32[4,64,128]{2,1,0:T(8,128)S(1)}, f32[68,8...) custom-call(f32[64,64,128]{2,1,0:T(8,128)S(1)} %copy-done, f32[64,64,128]{2,1,0:T(8,128)S(1)} %copy-done.1), custom_call_target="tpu_custom_call" | custom-call | flops 20000000 | bytes 4000000 | tf_op jit(solution)/shard_map/faces/pallas_call | solution.py:143
  9.0 4.3 %collective-permute-start.2 = (f32[2,64,128]{2,1,0:T(8,128)S(1)}, f32[2,64,128]{2,1,0:T(8,128)S(1)}, u32[]{:S(2)}, u32[]{:S(2)}) collective-permute-start(f32[2,64,128]{2,1,0:T(8,128)S(1)} %get-tuple-element.30), channel_id=1, source_target_pairs={{0,1},{1,2},{2,3},{3,4},{4,5},{5,6},{6,7},{8,9},{9,10},{10,11},{11... | collective-permute-start | bytes 196616 | tf_op jit(solution)/shard_map/ppermute | solution.py:586
  13.3 0.0 copy-done.4
  13.3 0.0 copy-done.5
  13.4 0.4 bend.1
  13.8 0.0 copy-done.8
  13.8 0.0 copy-start.2
  13.8 0.0 copy-start.3
  13.8 0.0 copy-start.6
  13.8 0.0 copy-start.7
  13.9 0.0 copy-start.9
  13.9 3.3 %interior.1 = (f32[12,48,128]{2,1,0:T(8,128)S(1)}, f32[6,24,128]{2,1,0:T(8,128)S(1)}) custom-call(f32[68,80,128]{2,1,0:T(8,128)S(1)} %get-tuple-element.21.s_ref, f32[68,80,128]{2,1,0:T(8,128)S(1)} %get-tuple-element.22.t_ref, f32[64,64,128]{2,1,0:T(8,128)S(1)} %get-tuple-element.23.d_ref, bf16[48,128]{1,0:T(8,128)(2,1)S(1)} %copy-done.8), custom_call_target="tpu_custom_call" | custom-call | flops 40000000 | bytes 4000000 | tf_op jit(solution)/shard_map/interior/pallas_call | solution.py:313
  17.2 0.0 collective-permute-done.2.zr_ref
  17.2 0.0 collective-permute-done.xr_ref
  17.2 0.0 collective-permute-done.1.yr_ref
  17.2 0.0 copy-done.2
  17.2 0.0 copy-done.3
  17.2 0.0 copy-done.6
  17.2 0.0 copy-done.7
  17.2 0.0 copy-done.9
  17.2 0.9 %finish.1 = (f32[8,40,128]{2,1,0:T(8,128)S(1)}, f32[48,256]{1,0:T(8,128)S(1)}) custom-call(f32[12,48,128]{2,1,0:T(8,128)S(1)} %get-tuple-element.24.af_ref, f32[6,24,128]{2,1,0:T(8,128)S(1)} %get-tuple-element.25.ac_ref, f32[4,64,128]{2,1,0:T(8,128)S(1)} %collective-permute-done.xr_ref, f32[4,64,128]{2,1,0:T(8,128)S(1)} %get-tuple-element.27.xo_ref, ...), custom_call_target="tpu_custom_call" | custom-call | tf_op jit(solution)/shard_map/finish/pallas_call | solution.py:414
  18.2 10.0 %all_to_all.15.got_ref = f32[8,40,128]{2,1,0:T(8,128)S(1)} all-to-all(f32[8,40,128]{2,1,0:T(8,128)S(1)} %get-tuple-element.34), channel_id=1, replica_groups=mesh['gx'=8,'gy'=8,'gz'=8] {'gx'}, dimensions={0} | all-to-all | bytes 327680 | tf_op jit(solution)/shard_map/all_to_all | solution.py:590
  28.1 0.2 xstage.1
  28.3 15.5 %all_to_all.16.got_ref = f32[8,40,128]{2,1,0:T(8,128)S(1)} all-to-all(f32[8,40,128]{2,1,0:T(8,128)S(1)} %get-tuple-element.36), channel_id=1, replica_groups=mesh['gx'=8,'gy'=8,'gz'=8] {'gy'}, dimensions={0} | all-to-all | bytes 327680 | tf_op jit(solution)/shard_map/all_to_all | solution.py:590
  43.8 0.2 ystage.1
  44.0 19.7 %all_to_all.17.got_ref = f32[8,56,128]{2,1,0:T(8,128)S(1)} all-to-all(f32[8,56,128]{2,1,0:T(8,128)S(1)} %get-tuple-element.38), channel_id=1, replica_groups=mesh['gx'=8,'gy'=8,'gz'=8] {'gz'}, dimensions={0} | all-to-all | bytes 458752 | tf_op jit(solution)/shard_map/all_to_all | solution.py:590
  63.8 1.4 %zstage.1 = (f32[3,8,8,16]{3,2,1,0:T(8,128)}, f32[3,16,16,32]{3,2,1,0:T(8,128)}) custom-call(f32[8,56,128]{2,1,0:T(8,128)S(1)} %all_to_all.17.got_ref, f32[48,256]{1,0:T(8,128)S(1)} %get-tuple-element.39.fine_ref), custom_call_target="tpu_custom_call" | custom-call | tf_op jit(solution)/shard_map/zstage/pallas_call | solution.py:572
Async XLA Ops:
  0.6 7.1 %copy-start = (f32[64,64,128]{2,1,0:T(8,128)S(1)}, f32[64,64,128]{2,1,0:T(8,128)}, u32[]{:S(2)}) copy-start(f32[64,64,128]{2,1,0:T(8,128)} %w_hbm.1) | copy-start | bytes 6291460
  0.6 7.1 %copy-start.1 = (f32[64,64,128]{2,1,0:T(8,128)S(1)}, f32[64,64,128]{2,1,0:T(8,128)}, u32[]{:S(2)}) copy-start(f32[64,64,128]{2,1,0:T(8,128)} %f_hbm.1) | copy-start | bytes 6291460
  2.0 15.2 %collective-permute-start = (f32[4,64,128]{2,1,0:T(8,128)S(1)}, f32[4,64,128]{2,1,0:T(8,128)S(1)}, u32[]{:S(2)}, u32[]{:S(2)}) collective-permute-start(f32[4,64,128]{2,1,0:T(8,128)S(1)} %get-tuple-element.26), channel_id=1, source_target_pairs={{0,64},{64,128},{128,192},{192,256},{256,320},{320,384},{384,448},... | collective-permute-start | bytes 393224 | tf_op jit(solution)/shard_map/ppermute | solution.py:586
  4.0 9.3 %copy-start.4 = (f32[3,16,16,32]{3,2,1,0:T(8,128)S(1)}, f32[3,16,16,32]{3,2,1,0:T(8,128)}, u32[]{:S(2)}) copy-start(f32[3,16,16,32]{3,2,1,0:T(8,128)} %k_ref.1) | copy-start | bytes 294916
  4.1 9.3 %copy-start.5 = (f32[3,8,8,16]{3,2,1,0:T(8,128)S(1)}, f32[3,8,8,16]{3,2,1,0:T(8,128)}, u32[]{:S(2)}) copy-start(f32[3,8,8,16]{3,2,1,0:T(8,128)} %c_ref.1) | copy-start | bytes 36868
  4.1 9.7 %copy-start.8 = (bf16[48,128]{1,0:T(8,128)(2,1)S(1)}, bf16[48,128]{1,0:T(8,128)(2,1)}, u32[]{:S(2)}) copy-start(bf16[48,128]{1,0:T(8,128)(2,1)} %constant.12.clone.left_ref) | copy-start | bytes 36868
  4.1 13.1 %collective-permute-start.1 = (f32[4,64,128]{2,1,0:T(8,128)S(1)}, f32[4,64,128]{2,1,0:T(8,128)S(1)}, u32[]{:S(2)}, u32[]{:S(2)}) collective-permute-start(f32[4,64,128]{2,1,0:T(8,128)S(1)} %get-tuple-element.28), channel_id=1, source_target_pairs={{0,8},{8,16},{16,24},{24,32},{32,40},{40,48},{48,56},{1,9},{9,17},... | collective-permute-start | bytes 393224 | tf_op jit(solution)/shard_map/ppermute | solution.py:586
  9.0 8.1 %collective-permute-start.2 = (f32[2,64,128]{2,1,0:T(8,128)S(1)}, f32[2,64,128]{2,1,0:T(8,128)S(1)}, u32[]{:S(2)}, u32[]{:S(2)}) collective-permute-start(f32[2,64,128]{2,1,0:T(8,128)S(1)} %get-tuple-element.30), channel_id=1, source_target_pairs={{0,1},{1,2},{2,3},{3,4},{4,5},{5,6},{6,7},{8,9},{9,10},{10,11},{11... | collective-permute-start | bytes 196616 | tf_op jit(solution)/shard_map/ppermute | solution.py:586
  13.8 3.4 %copy-start.2 = (bf16[4,128,384]{2,1,0:T(8,128)(2,1)S(1)}, bf16[4,128,384]{2,1,0:T(8,128)(2,1)}, u32[]{:S(2)}) copy-start(bf16[4,128,384]{2,1,0:T(8,128)(2,1)} %constant.16.clone.mh_ref) | copy-start | bytes 1179652
  13.8 3.4 %copy-start.3 = (bf16[4,128,384]{2,1,0:T(8,128)(2,1)S(1)}, bf16[4,128,384]{2,1,0:T(8,128)(2,1)}, u32[]{:S(2)}) copy-start(bf16[4,128,384]{2,1,0:T(8,128)(2,1)} %constant.17.clone.ml_ref) | copy-start | bytes 1179652
  13.8 3.4 %copy-start.6 = (bf16[2,128,128]{2,1,0:T(8,128)(2,1)S(1)}, bf16[2,128,128]{2,1,0:T(8,128)(2,1)}, u32[]{:S(2)}) copy-start(bf16[2,128,128]{2,1,0:T(8,128)(2,1)} %constant.14.clone.wzh_ref) | copy-start | bytes 196612
  13.8 3.4 %copy-start.7 = (bf16[2,128,128]{2,1,0:T(8,128)(2,1)S(1)}, bf16[2,128,128]{2,1,0:T(8,128)(2,1)}, u32[]{:S(2)}) copy-start(bf16[2,128,128]{2,1,0:T(8,128)(2,1)} %constant.15.clone.wzl_ref) | copy-start | bytes 196612
  13.9 3.4 %copy-start.9 = (f32[8,8,128]{2,1,0:T(8,128)S(1)}, f32[8,8,128]{2,1,0:T(8,128)}, u32[]{:S(2)}) copy-start(f32[8,8,128]{2,1,0:T(8,128)} %constant.13.clone.wc_ref) | copy-start | bytes 98308
